TPU v7x, 16 devices: a whole 2x2x2 slice. The times are simulated.
16 devices in a mesh: data: 16 (over z, y, x, core).
Axes of the slice: x: 2, y: 2, z: 2, core: 2. Of those that a mesh axis runs over, the one named last changes fastest.
Arguments:
- grad_qkv: bfloat16 [16, 3, 1769472], P('data')
- weight_qkv: float32 [3, 1769472], P(None, 'data')
- mom_qkv: float32 [3, 1769472], P(None, 'data')
- var_qkv: float32 [3, 1769472], P(None, 'data')
- grad_proj: bfloat16 [16, 3, 589824], P('data')
- weight_proj: float32 [3, 589824], P(None, 'data')
- mom_proj: float32 [3, 589824], P(None, 'data')
- var_proj: float32 [3, 589824], P(None, 'data')
- grad_fc_in: bfloat16 [16, 3, 2359296], P('data')
- weight_fc_in: float32 [3, 2359296], P(None, 'data')
- mom_fc_in: float32 [3, 2359296], P(None, 'data')
- var_fc_in: float32 [3, 2359296], P(None, 'data')
- grad_fc_out: bfloat16 [16, 3, 2359296], P('data')
- weight_fc_out: float32 [3, 2359296], P(None, 'data')
- mom_fc_out: float32 [3, 2359296], P(None, 'data')
- var_fc_out: float32 [3, 2359296], P(None, 'data')
Outputs:
- output 1: bfloat16 [3, 1769472], replicated
- output 2: float32 [3, 1769472], P(None, 'data')
- output 3: float32 [3, 1769472], P(None, 'data')
- output 4: float32 [3, 1769472], P(None, 'data')
- output 5: bfloat16 [3, 589824], replicated
- output 6: float32 [3, 589824], P(None, 'data')
- output 7: float32 [3, 589824], P(None, 'data')
- output 8: float32 [3, 589824], P(None, 'data')
- output 9: bfloat16 [3, 2359296], replicated
- output 10: float32 [3, 2359296], P(None, 'data')
- output 11: float32 [3, 2359296], P(None, 'data')
- output 12: float32 [3, 2359296], P(None, 'data')
- output 13: bfloat16 [3, 2359296], replicated
- output 14: float32 [3, 2359296], P(None, 'data')
- output 15: float32 [3, 2359296], P(None, 'data')
- output 16: float32 [3, 2359296], P(None, 'data')
All inputs are finite; a program needn't handle non-finite values.
Results may differ from a plain program's by a relative error of at most 0.001.
Values are sent between devices in bfloat16 or wider.
A program may use at most 1 GiB of HBM per device.

v0:
```python
import functools

import jax
import jax.numpy as jnp
from jax import lax
from jax.experimental import pallas as pl
from jax.experimental.pallas import tpu as pltpu
from jax.sharding import PartitionSpec as P


STEP = 10
LEARN_RATE = 0.1
BETA_ONE = 0.9
BETA_TWO = 0.999
EPSILON = 1e-6
WEIGHT_DECAY = 0.01

MESH = pl.DeviceIdType.MESH
CHUNK = 12288
INNER = 1024
PACKED = CHUNK * 3 // 4
THIRD = PACKED // 3
PART = CHUNK // 3
SLOTS = 4
LEAD = 2
KINDS = (2, 3, 0, 1)
COUNTS = (12, 12, 9, 3)
STARTS = (0, 12, 24, 33)
TOTAL = 36
MOVED = 15
STEP_VMEM = 28 << 20
LAST_VMEM = 13 << 20
FAR_VMEM = 6 << 20
PACK_AT = 17
GROUP = 3
DEPTH = 12
RING = 4
ORDERS = ((0, 1, 2), (1, 2, 0), (2, 0, 1))


def kind_of(chunk):
    return sum(jnp.where(chunk >= start, 1, 0) for start in STARTS[1:])


def step_kernel(*refs):
    states, refs = refs[:16], refs[16:]
    (gathered, near_0, near_1, near_2, mate, wv, mv, vv,
     own, peer, pair, send1, keep, recv1, recv2, recv3, uv, acc, part, parts, ratio, quad, packed,
     own_sem, peer_send, peer_recv, s1, r1, s2, r2, s3, r3, state_sem, part_send, part_recv,
     a1s, a2s, a3s, a1r, a2r, a3r, self_sem, mate_send, mate_recv, a2n, near_send, near_recv) = refs
    near = (near_0, near_1, near_2)
    me = lax.axis_index("data")
    core = me % 2
    bits = ((me // 2) % 2, (me // 4) % 2, (me // 8) % 2)
    partner = me + 1 - 2 * core
    neighbour = tuple(me + (2 << d) * (1 - 2 * bits[d]) for d in range(3))

    def owner(rel, parity):
        index = parity
        for d in range(3):
            index = index + (2 << d) * (1 - bits[d] if (rel >> d) & 1 else bits[d])
        return index

    def remote(src, dst, ssem, rsem, device):
        return pltpu.make_async_remote_copy(src_ref=src, dst_ref=dst, send_sem=ssem, recv_sem=rsem,
                                            device_id=(device,), device_id_type=MESH)

    def wait_for(ref, sem):
        pltpu.make_async_copy(ref, ref, sem).wait()

    def slot_of(chunk):
        return lax.rem(chunk, SLOTS)

    def for_kind(chunk, body):
        for kind in range(4):
            @pl.when((chunk >= STARTS[kind]) & (chunk < STARTS[kind] + COUNTS[kind]))
            def _(kind=kind):
                body(kind, chunk - STARTS[kind])

    def load_own(chunk):
        def body(kind, local):
            width = COUNTS[kind] * CHUNK
            slot = slot_of(chunk)
            for rel in range(8):
                cols = pl.ds(pl.multiple_of(owner(rel, core) * width + local * CHUNK, 128), CHUNK)
                pltpu.make_async_copy(states[4 * kind].at[:, cols], own.at[slot, rel], own_sem.at[slot]).start()

        for_kind(chunk, body)

    def give_peer(chunk):
        def body(kind, local):
            width = COUNTS[kind] * CHUNK
            slot = slot_of(chunk)
            for rel in range(8):
                cols = pl.ds(pl.multiple_of(owner(rel, 1 - core) * width + local * CHUNK, 128), CHUNK)
                remote(states[4 * kind].at[:, cols], peer.at[slot, rel], peer_send.at[slot], peer_recv.at[slot], partner).start()

        for_kind(chunk, body)

    def pair_stage(chunk):
        slot = slot_of(chunk)
        wait_for(own.at[slot], own_sem.at[slot])
        wait_for(peer.at[slot], peer_recv.at[slot])

        @pl.when(chunk >= SLOTS)
        def _():
            wait_for(send1.at[slot], s1.at[slot])
            wait_for(recv2.at[slot], s2.at[slot])
            wait_for(recv3.at[slot], s3.at[slot])

        for rel in range(8):
            def inner(i, _, rel=rel):
                cols = pl.ds(pl.multiple_of(i * INNER, INNER), INNER)
                pair[rel] = own[slot, rel, :, cols].astype(jnp.float32) + peer[slot, rel, :, cols].astype(jnp.float32)
                for row in range(3):
                    a, b, c = ((rel >> d) & 1 for d in ORDERS[row])
                    dst = send1 if a else keep
                    dst[slot, row, 2 * b + c, :, cols] = pair[rel, row:row + 1, :]
                return 0

            lax.fori_loop(0, CHUNK // INNER, inner, 0)
        for row in range(3):
            remote(send1.at[slot, row], recv1.at[slot, row], s1.at[slot], r1.at[slot], neighbour[ORDERS[row][0]]).start()

    def prefetch(chunk):
        @pl.when(chunk >= SLOTS)
        def _():
            wait_for(peer.at[slot_of(chunk)], peer_send.at[slot_of(chunk)])

        load_own(chunk)
        give_peer(chunk)

    def add_stage(slot, recv, rsem, count):
        wait_for(recv.at[slot], rsem.at[slot])

        def inner(i, _):
            cols = pl.ds(pl.multiple_of(i * INNER, INNER), INNER)
            for row in range(3):
                for k in range(count):
                    keep[slot, row, k, :, cols] = keep[slot, row, k, :, cols] + recv[slot, row, k, :, cols]
            return 0

        lax.fori_loop(0, CHUNK // INNER, inner, 0)

    def second_stage(chunk):
        slot = slot_of(chunk)
        add_stage(slot, recv1, r1, 4)
        for row in range(3):
            remote(keep.at[slot, row, pl.ds(2, 2)], recv2.at[slot, row], s2.at[slot], r2.at[slot], neighbour[ORDERS[row][1]]).start()

    def third_stage(chunk):
        slot = slot_of(chunk)
        add_stage(slot, recv2, r2, 2)
        for row in range(3):
            remote(keep.at[slot, row, pl.ds(1, 1)], recv3.at[slot, row], s3.at[slot], r3.at[slot], neighbour[ORDERS[row][2]]).start()

    def last_stage(chunk):
        slot = slot_of(chunk)
        kind = kind_of(chunk)
        wait_for(recv3.at[slot], r3.at[slot])

        def inner(i, _):
            cols = pl.ds(pl.multiple_of(i * INNER, INNER), INNER)
            for row in range(3):
                line = slice(row, row + 1)
                mean = (keep[slot, row, 0, :, cols] + recv3[slot, row, 0, :, cols]) / 16
                weight = wv[chunk, line, cols]
                new_first = BETA_ONE * mv[chunk, line, cols] + (1.0 - BETA_ONE) * mean
                new_second = BETA_TWO * vv[chunk, line, cols] + (1.0 - BETA_TWO) * mean * mean
                direction = (new_first / (1.0 - BETA_ONE ** STEP)) / (jnp.sqrt(new_second / (1.0 - BETA_TWO ** STEP)) + EPSILON) + WEIGHT_DECAY * weight
                mv[chunk, line, cols] = new_first
                vv[chunk, line, cols] = new_second
                uv[chunk, row, :, cols] = direction
                acc[kind, row] += weight * weight
                acc[kind, 3 + row] += direction * direction
            return 0

        lax.fori_loop(0, CHUNK // INNER, inner, 0)

    def send_norms(kind):
        for j in range(6):
            part[kind, j:j + 1, :] = jnp.broadcast_to(jnp.sum(acc[kind, j], axis=1, keepdims=True), (1, 128))
        for j in range(6, 8):
            part[kind, j:j + 1, :] = jnp.zeros((1, 128), jnp.float32)
        parts[kind, me] = part[kind]
        for k in range(1, 16):
            remote(part.at[kind], parts.at[kind, me], part_send.at[kind], part_recv.at[kind], (me + k) % 16).start()

    def take_norms(kind):
        wait_for(parts.at[kind, pl.ds(0, 15)], part_recv.at[kind])
        total = parts[kind, 0]
        for i in range(1, 16):
            total = total + parts[kind, i]
        norms = jnp.sqrt(total)
        trust = norms[0:3, :] / norms[3:6, :]
        for row in range(3):
            for i in range(INNER // 128):
                ratio[kind, row, :, i * 128:(i + 1) * 128] = trust[row:row + 1, :]

    def update(chunk):
        kind = kind_of(chunk)

        def inner(i, _):
            cols = pl.ds(pl.multiple_of(i * INNER, INNER), INNER)
            for row in range(3):
                line = slice(row, row + 1)
                wv[chunk, line, cols] = wv[chunk, line, cols] - LEARN_RATE * ratio[kind, row] * uv[chunk, row, :, cols]
            return 0

        lax.fori_loop(0, CHUNK // INNER, inner, 0)

    def pack(unit):
        begin = lax.rem(unit, GROUP) * PART
        for k in range(3):
            chunk = unit - lax.rem(unit, GROUP) + k
            for row in range(3):
                head = pl.ds(pl.multiple_of(begin + row * INNER, INNER), INNER)
                tail = pl.ds(pl.multiple_of(begin + THIRD, INNER), INNER)
                quad[row, 0:3, :] = wv[chunk, :, head]
                quad[row, 3:4, :] = wv[chunk, row:row + 1, tail]
                packed[unit, :, k * THIRD + row * INNER:k * THIRD + (row + 1) * INNER] = quad[row].astype(jnp.bfloat16)

    def thirds(k):
        return pl.ds(k * THIRD, THIRD)

    def offset(*dims):
        return sum(1 << d for d in dims)

    def piece(rel, chunk, k):
        return gathered.at[owner(rel, core), chunk - MOVED, :, thirds(k)]

    def to_partner(rel, chunk, k):
        remote(piece(rel, chunk, k), piece(rel, chunk, k), mate_send, mate_recv, partner).start()

    def near_to_partner(k, j, chunk):
        remote(near[k].at[j, chunk], mate.at[k, j, chunk], near_send, near_recv, partner).start()

    def gather_one(chunk):
        slot = slot_of(chunk)

        @pl.when(chunk < MOVED)
        def _():
            for k in range(3):
                mine = packed.at[chunk, :, thirds(k)]
                remote(mine, near[k].at[1, chunk], a1s, a1r.at[slot], neighbour[ORDERS[k][0]]).start()
                remote(mine, mate.at[k, 0, chunk], near_send, near_recv, partner).start()
                pltpu.make_async_copy(mine, near[k].at[0, chunk], self_sem).start()

        @pl.when(chunk >= MOVED)
        def _():
            for k in range(3):
                remote(packed.at[chunk, :, thirds(k)], piece(0, chunk, k), a1s, a1r.at[slot], neighbour[ORDERS[k][0]]).start()
            mine = gathered.at[me, chunk - MOVED]
            remote(packed.at[chunk], mine, mate_send, mate_recv, partner).start()
            pltpu.make_async_copy(packed.at[chunk], mine, self_sem).start()

    def gather_two(chunk):
        slot = slot_of(chunk)
        wait_for(packed.at[0], a1r.at[slot])

        @pl.when(chunk < MOVED)
        def _():
            for k in range(3):
                device = neighbour[ORDERS[k][1]]
                remote(packed.at[chunk, :, thirds(k)], near[k].at[2, chunk], a2n, a2r.at[slot], device).start()
                remote(near[k].at[1, chunk], near[k].at[3, chunk], a2n, a2r.at[slot], device).start()
            for k in range(3):
                near_to_partner(k, 1, chunk)

        @pl.when(chunk >= MOVED)
        def _():
            for k in range(3):
                a, b, _ = ORDERS[k]
                remote(packed.at[chunk, :, thirds(k)], piece(0, chunk, k), a2s, a2r.at[slot], neighbour[b]).start()
                remote(piece(offset(a), chunk, k), piece(offset(a), chunk, k), a2s, a2r.at[slot], neighbour[b]).start()
            for k in range(3):
                to_partner(offset(ORDERS[k][0]), chunk, k)

    def gather_three(chunk):
        slot = slot_of(chunk)
        wait_for(packed.at[pl.ds(0, 2)], a2r.at[slot])

        @pl.when(chunk < MOVED)
        def _():
            for k in range(3):
                near_to_partner(k, 2, chunk)
                near_to_partner(k, 3, chunk)

        @pl.when(chunk >= MOVED)
        def _():
            for k in range(3):
                a, b, c = ORDERS[k]
                remote(packed.at[chunk, :, thirds(k)], piece(0, chunk, k), a3s, a3r.at[slot], neighbour[c]).start()
                for rel in (offset(a), offset(b), offset(a, b)):
                    remote(piece(rel, chunk, k), piece(rel, chunk, k), a3s, a3r.at[slot], neighbour[c]).start()
            for k in range(3):
                a, b, c = ORDERS[k]
                to_partner(offset(b), chunk, k)
                to_partner(offset(a, b), chunk, k)

    def gather_four(chunk):
        @pl.when(chunk >= MOVED)
        def _():
            wait_for(packed.at[pl.ds(0, 4)], a3r.at[slot_of(chunk)])
            for k in range(3):
                a, b, c = ORDERS[k]
                for rel in (offset(c), offset(a, c), offset(b, c), offset(a, b, c)):
                    to_partner(rel, chunk, k)

    def at_chunk(chunk, body):
        @pl.when((chunk >= 0) & (chunk < TOTAL))
        def _():
            body(chunk)

    load_own(jnp.int32(0))
    load_own(jnp.int32(1))
    barrier = pltpu.get_barrier_semaphore()
    for k in range(1, 16):
        pl.semaphore_signal(barrier, inc=1, device_id=((me + k) % 16,), device_id_type=MESH)
    pl.semaphore_wait(barrier, 15)
    give_peer(jnp.int32(0))
    give_peer(jnp.int32(1))
    acc[...] = jnp.zeros_like(acc)

    def step(s, _):
        at_chunk(s, pair_stage)

        @pl.when(s + LEAD < TOTAL)
        def _():
            prefetch(s + LEAD)

        @pl.when(s == 0)
        def _():
            for kind in range(4):
                def load_states(i, _, kind=kind):
                    cols = pl.ds(pl.multiple_of(i * CHUNK, CHUNK), CHUNK)
                    for j, dst in enumerate((wv, mv, vv)):
                        pltpu.make_async_copy(states[4 * kind + 1 + j].at[:, cols], dst.at[STARTS[kind] + i], state_sem.at[j]).start()
                    return 0

                lax.fori_loop(0, COUNTS[kind], load_states, 0)

        at_chunk(s - 1, second_stage)
        at_chunk(s - 2, third_stage)

        @pl.when(s == 3)
        def _():
            for j, dst in enumerate((wv, mv, vv)):
                wait_for(dst, state_sem.at[j])

        at_chunk(s - 3, last_stage)
        for kind in range(4):
            @pl.when(s == STARTS[kind] + COUNTS[kind] + 2)
            def _(kind=kind):
                send_norms(kind)

            @pl.when(s == PACK_AT - 2 + STARTS[kind])
            def _(kind=kind):
                take_norms(kind)
        at_chunk(s - PACK_AT - 1, gather_one)
        at_chunk(s - PACK_AT - 2, gather_two)
        at_chunk(s - PACK_AT - 3, gather_three)
        at_chunk(s - PACK_AT - 4, gather_four)
        at_chunk(s - PACK_AT + 2, update)
        at_chunk(s - PACK_AT, pack)
        return 0

    lax.fori_loop(0, TOTAL + PACK_AT + 5, step, 0)

    def drain(chunk, _):
        slot = slot_of(chunk)
        wait_for(peer.at[slot], peer_send.at[slot])
        wait_for(send1.at[slot], s1.at[slot])
        wait_for(recv2.at[slot], s2.at[slot])
        wait_for(recv3.at[slot], s3.at[slot])
        return 0

    lax.fori_loop(TOTAL - SLOTS, TOTAL, drain, 0)
    for kind in range(4):
        wait_for(parts.at[kind, pl.ds(0, 15)], part_send.at[kind])
    wait_for(packed, a1s)
    wait_for(packed, self_sem)
    wait_for(gathered.at[pl.ds(0, 2)], a2s)
    wait_for(mate.at[:, pl.ds(0, 2)], a2n)
    wait_for(gathered.at[pl.ds(0, 4)], a3s)
    for sem in (mate_send, mate_recv):
        wait_for(gathered.at[pl.ds(0, 8)], sem)
    for sem in (near_send, near_recv):
        wait_for(mate, sem)


def wait_for(ref, sem):
    pltpu.make_async_copy(ref, ref, sem).wait()


def in_vmem(x):
    return pltpu.with_memory_space_constraint(x, pltpu.VMEM)


def unpack_part(src, dst, col, rows):
    dst[:, pl.ds(col, THIRD)] = src[0:3, :]
    for row in range(3):
        rows[row:row + 1, :] = src[3:4, row * INNER:(row + 1) * INNER].astype(jnp.float32)
    dst[:, pl.ds(col + THIRD, INNER)] = rows[...].astype(jnp.bfloat16)


class MovedRing:
    def __init__(self, sources, far, outs, buffers):
        self.sources, self.far, self.outs = sources, far, outs
        self.full, self.rows, self.store_sem = buffers
        self.groups = MOVED // GROUP
        self.steps = 4 * self.groups
        me = lax.axis_index("data")
        self.core = me % 2
        self.bits = ((me // 2) % 2, (me // 4) % 2, (me // 8) % 2)

    def store(self, step):
        slot = lax.rem(step, RING)
        j, group = step // self.groups, lax.rem(step, self.groups)
        for i, (_, k, other) in enumerate(self.sources):
            rel = [0, 0, 0]
            for d, bit in zip(ORDERS[k], (j % 2, j // 2, self.far)):
                rel[d] = bit
            shard = self.core + other - 2 * other * self.core
            for d in range(3):
                shard = shard + (2 << d) * (self.bits[d] + rel[d] - 2 * self.bits[d] * rel[d])
            for kind in range(2):
                @pl.when((group >= COUNTS[0] // GROUP) if kind else (group < COUNTS[0] // GROUP))
                def _(kind=kind, i=i, k=k, shard=shard):
                    begin = (shard * COUNTS[kind] + group * GROUP + k - STARTS[kind]) * CHUNK
                    pltpu.make_async_copy(self.full.at[slot, i], self.outs[kind].at[:, pl.ds(pl.multiple_of(begin, CHUNK), CHUNK)],
                                          self.store_sem.at[slot]).start()

    def run(self):
        def body(step, _):
            slot = lax.rem(step, RING)

            @pl.when(step >= RING)
            def _():
                wait_for(self.full.at[slot], self.store_sem.at[slot])

            j, first = step // self.groups, lax.rem(step, self.groups) * GROUP
            for i, (source, _, _) in enumerate(self.sources):
                for c in range(GROUP):
                    unpack_part(source.at[j, first + c], self.full.at[slot, i], c * PART, self.rows.at[c])
            self.store(step)
            return 0

        lax.fori_loop(0, self.steps, body, 0)

    def drain(self):
        for slot in range(RING):
            wait_for(self.full.at[slot], self.store_sem.at[slot])

    @staticmethod
    def scratch(count):
        return [pltpu.VMEM((RING, count, 3, CHUNK), jnp.bfloat16), pltpu.VMEM((GROUP, 3, INNER), jnp.float32), pltpu.SemaphoreType.DMA((RING,))]


def finish_kernel(gathered, near_0, near_1, near_2, mate, wv, mv, vv, *refs):
    outs, refs = refs[:16], refs[16:]
    packed, full, load_sem, store_sem, out_sem = refs[:5]
    units = 16 * ((TOTAL - MOVED) // GROUP)
    sources = [(ref, k, 0) for k, ref in enumerate((near_0, near_1, near_2))]
    sources += [(mate.at[k], k, 1) for k in range(3)]
    moved = MovedRing(sources, 0, (outs[0], outs[4]), refs[5:])
    rows = moved.rows

    def load(unit):
        slot = lax.rem(unit, DEPTH)
        pltpu.make_async_copy(gathered.at[unit % 16, pl.ds((unit // 16) * GROUP, GROUP)], packed.at[slot], load_sem.at[slot]).start()

    def store(unit):
        slot = lax.rem(unit, DEPTH)
        first = (unit // 16) * GROUP + MOVED
        for kind in range(1, 4):
            @pl.when((first >= STARTS[kind]) & (first < STARTS[kind] + COUNTS[kind]))
            def _(kind=kind):
                begin = (unit % 16) * (COUNTS[kind] * CHUNK) + (first - STARTS[kind]) * CHUNK
                cols = pl.ds(pl.multiple_of(begin, CHUNK), GROUP * CHUNK)
                pltpu.make_async_copy(full.at[slot], outs[4 * kind].at[:, cols], store_sem.at[slot]).start()

    def unpack(slot):
        for i in range(GROUP):
            for k in range(3):
                unpack_part(packed.at[slot, i, :, pl.ds(k * THIRD, THIRD)], full.at[slot], k * CHUNK + i * PART, rows.at[k])

    def fill(unit, _):
        load(unit)
        return 0

    lax.fori_loop(0, DEPTH, fill, 0)
    for j, src in enumerate((wv, mv, vv)):
        for kind in range(4):
            def put(i, _, kind=kind, j=j, src=src):
                cols = pl.ds(pl.multiple_of(i * CHUNK, CHUNK), CHUNK)
                pltpu.make_async_copy(src.at[STARTS[kind] + i], outs[4 * kind + 1 + j].at[:, cols], out_sem.at[j]).start()
                return 0

            lax.fori_loop(0, COUNTS[kind], put, 0)

    def step(unit, _):
        slot = lax.rem(unit, DEPTH)
        wait_for(packed.at[slot], load_sem.at[slot])

        @pl.when(unit >= DEPTH)
        def _():
            wait_for(full.at[slot], store_sem.at[slot])

        unpack(slot)
        store(unit)

        @pl.when(unit + DEPTH < units)
        def _():
            load(unit + DEPTH)

        return 0

    lax.fori_loop(0, units, step, 0)
    moved.run()

    def drain(slot, _):
        wait_for(full.at[slot], store_sem.at[slot])
        return 0

    lax.fori_loop(0, DEPTH, drain, 0)
    moved.drain()
    for j, src in enumerate((wv, mv, vv)):
        wait_for(src, out_sem.at[j])


def finish(gathered, near, mate, new_states):
    f32, bf16 = jnp.float32, jnp.bfloat16
    dma = pltpu.SemaphoreType.DMA
    any_space = pl.BlockSpec(memory_space=pl.ANY)
    shapes = []
    for count in COUNTS:
        shapes += [jax.ShapeDtypeStruct((3, 16 * count * CHUNK), bf16)] + [jax.ShapeDtypeStruct((3, count * CHUNK), f32)] * 3
    return pl.pallas_call(
        finish_kernel,
        out_shape=tuple(shapes),
        in_specs=[any_space] + [pl.BlockSpec(memory_space=pltpu.VMEM)] * 7,
        out_specs=(any_space,) * 16,
        scratch_shapes=[
            pltpu.VMEM((DEPTH, GROUP, 4, PACKED), bf16), pltpu.VMEM((DEPTH, 3, GROUP * CHUNK), bf16),
            dma((DEPTH,)), dma((DEPTH,)), dma((3,)),
        ] + MovedRing.scratch(6),
        compiler_params=pltpu.CompilerParams(vmem_limit_bytes=LAST_VMEM),
        cost_estimate=pl.CostEstimate(flops=10 ** 12, bytes_accessed=10 ** 8, transcendentals=0),
        name="finish",
    )(pltpu.with_memory_space_constraint(gathered, pltpu.HBM), *[in_vmem(x) for x in (*near, mate, *new_states)])


def far_kernel(other, *refs):
    arrays, outs, buffers = refs[:3], refs[5:7], refs[7:]
    ring = MovedRing([(ref, k, other) for k, ref in enumerate(arrays)], 1, outs, buffers)
    ring.run()
    ring.drain()


def finish_far(far, other, copies):
    any_space = pl.BlockSpec(memory_space=pl.ANY)
    return pl.pallas_call(
        functools.partial(far_kernel, other),
        out_shape=tuple(jax.ShapeDtypeStruct(x.shape, x.dtype) for x in copies),
        in_specs=[pl.BlockSpec(memory_space=pltpu.VMEM)] * 3 + [any_space] * 2,
        out_specs=(any_space,) * 2,
        scratch_shapes=MovedRing.scratch(3),
        input_output_aliases={3: 0, 4: 1},
        compiler_params=pltpu.CompilerParams(vmem_limit_bytes=FAR_VMEM),
        cost_estimate=pl.CostEstimate(flops=10 ** 11, bytes_accessed=10 ** 7, transcendentals=0),
    )(*far, *copies)


def optimizer_step(blocks):
    f32, bf16 = jnp.float32, jnp.bfloat16
    dma = pltpu.SemaphoreType.DMA
    any_space = pl.BlockSpec(memory_space=pl.ANY)
    operands = []
    for kind in KINDS:
        grad, weight, first_mom, second_mom = blocks[4 * kind:4 * kind + 4]
        operands += [grad.reshape(grad.shape[1:]), weight, first_mom, second_mom]
    part = pltpu.VMEM((4, MOVED, 4, THIRD), bf16)
    state = pltpu.VMEM((TOTAL, 3, CHUNK), f32)
    vmem_space = pl.BlockSpec(memory_space=pltpu.VMEM)
    return pl.pallas_call(
        step_kernel,
        out_shape=(pltpu.HBM((16, TOTAL - MOVED, 4, PACKED), bf16), part, part, part, pltpu.VMEM((3,) + part.shape, bf16), state, state, state),
        in_specs=[any_space] * 16,
        out_specs=(any_space,) + (vmem_space,) * 7,
        scratch_shapes=[
            pltpu.VMEM((SLOTS, 8, 3, CHUNK), bf16), pltpu.VMEM((SLOTS, 8, 3, CHUNK), bf16), pltpu.VMEM((8, 3, INNER), f32),
            pltpu.VMEM((SLOTS, 3, 4, 1, CHUNK), f32), pltpu.VMEM((SLOTS, 3, 4, 1, CHUNK), f32),
            pltpu.VMEM((SLOTS, 3, 4, 1, CHUNK), f32), pltpu.VMEM((SLOTS, 3, 2, 1, CHUNK), f32), pltpu.VMEM((SLOTS, 3, 1, 1, CHUNK), f32),
            pltpu.VMEM((TOTAL, 3, 1, CHUNK), f32),
            pltpu.VMEM((4, 6, 1, INNER), f32), pltpu.VMEM((4, 8, 128), f32), pltpu.VMEM((4, 16, 8, 128), f32), pltpu.VMEM((4, 3, 1, INNER), f32),
            pltpu.VMEM((3, 4, INNER), f32), pltpu.VMEM((TOTAL, 4, PACKED), bf16),
            dma((SLOTS,)), dma((SLOTS,)), dma((SLOTS,)),
            dma((SLOTS,)), dma((SLOTS,)), dma((SLOTS,)), dma((SLOTS,)), dma((SLOTS,)), dma((SLOTS,)),
            dma((3,)), dma((4,)), dma((4,)),
            dma, dma, dma, dma((SLOTS,)), dma((SLOTS,)), dma((SLOTS,)), dma, dma, dma, dma, dma, dma,
        ],
        compiler_params=pltpu.CompilerParams(collective_id=0, has_side_effects=True, vmem_limit_bytes=STEP_VMEM),
        name="lamb_step",
    )(*operands)


def solution(mesh):
    grad_spec = P("data", None, None)
    shard_spec = P(None, "data")
    full_spec = P(None, None)

    def device_step(*blocks):
        gathered, *near_mate = optimizer_step(blocks)
        near, mate, new_states = near_mate[:3], near_mate[3], near_mate[4:]
        far = []
        for k in range(3):
            far.append(in_vmem(lax.ppermute(near[k], "data", [(i, i ^ (2 << ORDERS[k][2])) for i in range(16)])))
        outs = list(finish(gathered, near, mate, new_states))
        far_mate = []
        for k in range(3):
            far_mate.append(in_vmem(lax.ppermute(far[k], "data", [(i, i ^ 1) for i in range(16)])))
        copies = (outs[0], outs[4])
        copies = finish_far(far, 0, copies)
        outs[0], outs[4] = finish_far(far_mate, 1, copies)
        results = [None] * 16
        for slot, kind in enumerate(KINDS):
            results[4 * kind:4 * kind + 4] = outs[4 * slot:4 * slot + 4]
        return tuple(results)

    return jax.shard_map(device_step, mesh=mesh, in_specs=(grad_spec, shard_spec, shard_spec, shard_spec) * 4, out_specs=(full_spec, shard_spec, shard_spec, shard_spec) * 4, check_vma=False)
```

profile of v0, /device:TPU:0, one launch (start us, length us, event | category | flops | bytes accessed | tf_op | source)
XLA Modules:
  0.0 433.6 jit_solution(6555904617815892590)
XLA Ops:
  0.7 384.1 %lamb_step.1 = (bf16[16,21,4,9216]{3,2,1,0:T(4,128)(2,1)}, bf16[4,15,4,3072]{3,2,1,0:T(4,128)(2,1)}, bf16[4,15,4,3072]{3,2,1,0:T(4,128)(2,1)}, bf16[4,15,4,3072]...) custom-call(bf16[3,2359296]{1,0:T(4,128)(2,1)} %bitcast.4, ...), custom_call_target="tpu_custom_call" | custom-call | tf_op jit(solution)/shard_map/lamb_step/pallas_call | solution.py:586
  384.8 1.2 collective-permute-start
  386.0 0.8 collective-permute-start.2
  386.8 0.6 collective-permute-start.4
  387.5 34.0 %finish.1 = (bf16[3,2359296]{1,0:T(4,128)(2,1)}, f32[3,147456]{1,0:T(4,128)}, f32[3,147456]{1,0:T(4,128)}, f32[3,147456]{1,0:T(4,128)}, bf16[3,2359296]{1,0:T(4,...) custom-call(bf16[16,21,4,9216]{3,2,1,0:T(4,128)(2,1)} %get-tuple-ele, ...), custom_call_target="tpu_custom_call" | custom-call | flops 999999995904 | bytes 100000000 | tf_op jit(solution)/shard_map/finish/pallas_call | solution.py:539
  421.5 0.0 collective-permute-done.refs_0_
  421.5 0.0 collective-permute-start.1
  421.5 0.0 collective-permute-done.2.refs_1_
  421.5 0.5 collective-permute-start.3
  422.0 0.0 collective-permute-done.4.refs_2_
  422.0 0.1 collective-permute-start.5
  422.1 6.7 %shard_map.279 = (bf16[3,2359296]{1,0:T(4,128)(2,1)}, bf16[3,2359296]{1,0:T(4,128)(2,1)}) custom-call(bf16[4,15,4,3072]{3,2,1,0:T(4,128)(2,1)} %collective-permute-done.refs_0_, bf16[4,15,4,3072]{3,2,1,0:T(4,128)(2,1)} %collective-permute-done.2.refs_1_, ...), custom_call_target="tpu_custom_call", output_to_operand_aliasing={{0}: (3, {}), {1}: (4, {})} | custom-call | flops 99999997952 | bytes 10000000 | tf_op jit(solution)/shard_map/pallas_call | solution.py:563
  428.8 0.0 collective-permute-done.1.refs_0_
  428.8 0.0 collective-permute-done.3.refs_1_
  428.8 0.4 collective-permute-done.5.refs_2_
  429.2 4.4 %shard_map.280 = (bf16[3,2359296]{1,0:T(4,128)(2,1)}, bf16[3,2359296]{1,0:T(4,128)(2,1)}) custom-call(bf16[4,15,4,3072]{3,2,1,0:T(4,128)(2,1)S(1)} %collective-permute-done.1.refs_0_, bf16[4,15,4,3072]{3,2,1,0:T(4,128)(2,1)S(1)} %collective-permute-done.3.refs_1_, ...), custom_call_target="tpu_custom_call", output_to_operand_aliasing={{0}: (3, {}), {1}: (4, {})} | custom-call | flops 99999997952 | bytes 10000000 | tf_op jit(solution)/shard_map/pallas_call | solution.py:563
Async XLA Ops:
  384.8 36.7 %collective-permute-start = (bf16[4,15,4,3072]{3,2,1,0:T(4,128)(2,1)}, bf16[4,15,4,3072]{3,2,1,0:T(4,128)(2,1)}, u32[]{:S(2)}, u32[]{:S(2)}) collective-permute-start(bf16[4,15,4,3072]{3,2,1,0:T(4,128)(2,1)} %get-tuple-element.45.near_0), channel_id=1, source_target_pairs={{0,8},{1,9},{2,10},{3,11},{4,12},{5,13},{6,14},{7,15},{8,0},{9,1},... | collective-permute-start | bytes 4423688 | tf_op jit(solution)/shard_map/ppermute | solution.py:618
  386.0 35.5 %collective-permute-start.2 = (bf16[4,15,4,3072]{3,2,1,0:T(4,128)(2,1)}, bf16[4,15,4,3072]{3,2,1,0:T(4,128)(2,1)}, u32[]{:S(2)}, u32[]{:S(2)}) collective-permute-start(bf16[4,15,4,3072]{3,2,1,0:T(4,128)(2,1)} %get-tuple-element.46.near_1), channel_id=1, source_target_pairs={{0,2},{1,3},{2,0},{3,1},{4,6},{5,7},{6,4},{7,5},{8,10},{9,11},{10,... | collective-permute-start | bytes 4423688 | tf_op jit(solution)/shard_map/ppermute | solution.py:618
  386.8 35.2 %collective-permute-start.4 = (bf16[4,15,4,3072]{3,2,1,0:T(4,128)(2,1)}, bf16[4,15,4,3072]{3,2,1,0:T(4,128)(2,1)}, u32[]{:S(2)}, u32[]{:S(2)}) collective-permute-start(bf16[4,15,4,3072]{3,2,1,0:T(4,128)(2,1)} %get-tuple-element.47.near_2), channel_id=1, source_target_pairs={{0,4},{1,5},{2,6},{3,7},{4,0},{5,1},{6,2},{7,3},{8,12},{9,13},{10,... | collective-permute-start | bytes 4423688 | tf_op jit(solution)/shard_map/ppermute | solution.py:618
  421.5 7.3 %collective-permute-start.1 = (bf16[4,15,4,3072]{3,2,1,0:T(4,128)(2,1)}, bf16[4,15,4,3072]{3,2,1,0:T(4,128)(2,1)S(1)}, u32[]{:S(2)}, u32[]{:S(2)}) collective-permute-start(bf16[4,15,4,3072]{3,2,1,0:T(4,128)(2,1)} %collective-permute-done.refs_0_), channel_id=1, source_target_pairs={{0,1},{1,0},{2,3},{3,2},{4,5},{5,4},{6,7},{7,6},{8,9},{9,8},{10,11... | collective-permute-start | bytes 4423688 | tf_op jit(solution)/shard_map/ppermute | solution.py:622
  421.5 7.2 %collective-permute-start.3 = (bf16[4,15,4,3072]{3,2,1,0:T(4,128)(2,1)}, bf16[4,15,4,3072]{3,2,1,0:T(4,128)(2,1)S(1)}, u32[]{:S(2)}, u32[]{:S(2)}) collective-permute-start(bf16[4,15,4,3072]{3,2,1,0:T(4,128)(2,1)} %collective-permute-done.2.refs_1_), channel_id=1, source_target_pairs={{0,1},{1,0},{2,3},{3,2},{4,5},{5,4},{6,7},{7,6},{8,9},{9,8},{10,11... | collective-permute-start | bytes 4423688 | tf_op jit(solution)/shard_map/ppermute | solution.py:622
  422.0 7.2 %collective-permute-start.5 = (bf16[4,15,4,3072]{3,2,1,0:T(4,128)(2,1)}, bf16[4,15,4,3072]{3,2,1,0:T(4,128)(2,1)S(1)}, u32[]{:S(2)}, u32[]{:S(2)}) collective-permute-start(bf16[4,15,4,3072]{3,2,1,0:T(4,128)(2,1)} %collective-permute-done.4.refs_2_), channel_id=1, source_target_pairs={{0,1},{1,0},{2,3},{3,2},{4,5},{5,4},{6,7},{7,6},{8,9},{9,8},{10,11... | collective-permute-start | bytes 4423688 | tf_op jit(solution)/shard_map/ppermute | solution.py:622
where the time goes:
time: 434 us
  Pallas kernels  429 us (99%)
    pallas_call x1, Pallas kernels, optimizer_step(): pl.pallas_call(step_kernel, out_shape=(pltpu.HBM((16, TOTAL - MOVED, 4, P...  384 us
    pallas_call x1, Pallas kernels, finish(): pl.pallas_call(finish_kernel, out_shape=tuple(shapes), in_specs=[any_spac...  34 us
    pallas_call x2, Pallas kernels, finish_far(): pl.pallas_call(functools.partial(far_kernel, other), out_shape=tuple((jax...  11.1 us
  transfers between devices with their start and end apart: 6, of which 1 were waited for; matrix products, arithmetic and copies ran while one was open for 0% of the time, Pallas kernels for 9%

commit v1 on v0

--- a/solution.py
+++ b/solution.py
@@ -81,9 +81,10 @@
         def body(kind, local):
             width = COUNTS[kind] * CHUNK
             slot = slot_of(chunk)
-            for rel in range(8):
-                cols = pl.ds(pl.multiple_of(owner(rel, core) * width + local * CHUNK, 128), CHUNK)
-                pltpu.make_async_copy(states[4 * kind].at[:, cols], own.at[slot, rel], own_sem.at[slot]).start()
+            for i in range(3):
+                for rel in range(8):
+                    cols = pl.ds(pl.multiple_of(owner(rel, core) * width + local * CHUNK + i * PART, 128), PART)
+                    pltpu.make_async_copy(states[4 * kind].at[:, cols], own.at[slot, rel, :, pl.ds(i * PART, PART)], own_sem.at[slot, i]).start()
 
         for_kind(chunk, body)
 
@@ -91,16 +92,15 @@
         def body(kind, local):
             width = COUNTS[kind] * CHUNK
             slot = slot_of(chunk)
-            for rel in range(8):
-                cols = pl.ds(pl.multiple_of(owner(rel, 1 - core) * width + local * CHUNK, 128), CHUNK)
-                remote(states[4 * kind].at[:, cols], peer.at[slot, rel], peer_send.at[slot], peer_recv.at[slot], partner).start()
+            for i in range(3):
+                for rel in range(8):
+                    cols = pl.ds(pl.multiple_of(owner(rel, 1 - core) * width + local * CHUNK + i * PART, 128), PART)
+                    remote(states[4 * kind].at[:, cols], peer.at[slot, rel, :, pl.ds(i * PART, PART)], peer_send.at[slot], peer_recv.at[slot, i], partner).start()
 
         for_kind(chunk, body)
 
     def pair_stage(chunk):
         slot = slot_of(chunk)
-        wait_for(own.at[slot], own_sem.at[slot])
-        wait_for(peer.at[slot], peer_recv.at[slot])
 
         @pl.when(chunk >= SLOTS)
         def _():
@@ -108,19 +108,26 @@
             wait_for(recv2.at[slot], s2.at[slot])
             wait_for(recv3.at[slot], s3.at[slot])
 
-        for rel in range(8):
-            def inner(i, _, rel=rel):
-                cols = pl.ds(pl.multiple_of(i * INNER, INNER), INNER)
-                pair[rel] = own[slot, rel, :, cols].astype(jnp.float32) + peer[slot, rel, :, cols].astype(jnp.float32)
-                for row in range(3):
-                    a, b, c = ((rel >> d) & 1 for d in ORDERS[row])
-                    dst = send1 if a else keep
-                    dst[slot, row, 2 * b + c, :, cols] = pair[rel, row:row + 1, :]
-                return 0
-
-            lax.fori_loop(0, CHUNK // INNER, inner, 0)
-        for row in range(3):
-            remote(send1.at[slot, row], recv1.at[slot, row], s1.at[slot], r1.at[slot], neighbour[ORDERS[row][0]]).start()
+        def one_part(n, _):
+            cols = pl.ds(pl.multiple_of(n * PART, PART), PART)
+            wait_for(own.at[slot, :, :, cols], own_sem.at[slot, n])
+            wait_for(peer.at[slot, :, :, cols], peer_recv.at[slot, n])
+            for rel in range(8):
+                def inner(i, _, rel=rel):
+                    cols = pl.ds(pl.multiple_of(n * PART + i * INNER, INNER), INNER)
+                    pair[rel] = own[slot, rel, :, cols].astype(jnp.float32) + peer[slot, rel, :, cols].astype(jnp.float32)
+                    for row in range(3):
+                        a, b, c = ((rel >> d) & 1 for d in ORDERS[row])
+                        dst = send1 if a else keep
+                        dst[slot, row, 2 * b + c, :, cols] = pair[rel, row:row + 1, :]
+                    return 0
+
+                lax.fori_loop(0, PART // INNER, inner, 0)
+            for row in range(3):
+                remote(send1.at[slot, row, :, :, cols], recv1.at[slot, row, :, :, cols], s1.at[slot], r1.at[slot], neighbour[ORDERS[row][0]]).start()
+            return 0
+
+        lax.fori_loop(0, 3, one_part, 0)
 
     def prefetch(chunk):
         @pl.when(chunk >= SLOTS)
@@ -595,7 +602,7 @@
             pltpu.VMEM((TOTAL, 3, 1, CHUNK), f32),
             pltpu.VMEM((4, 6, 1, INNER), f32), pltpu.VMEM((4, 8, 128), f32), pltpu.VMEM((4, 16, 8, 128), f32), pltpu.VMEM((4, 3, 1, INNER), f32),
             pltpu.VMEM((3, 4, INNER), f32), pltpu.VMEM((TOTAL, 4, PACKED), bf16),
-            dma((SLOTS,)), dma((SLOTS,)), dma((SLOTS,)),
+            dma((SLOTS, 3)), dma((SLOTS,)), dma((SLOTS, 3)),
             dma((SLOTS,)), dma((SLOTS,)), dma((SLOTS,)), dma((SLOTS,)), dma((SLOTS,)), dma((SLOTS,)),
             dma((3,)), dma((4,)), dma((4,)),
             dma, dma, dma, dma((SLOTS,)), dma((SLOTS,)), dma((SLOTS,)), dma, dma, dma, dma, dma, dma,

time: 434 us -> 433 us (level)
  no operation moved by 1% of the time
where the time goes in v1:
time: 433 us; the launch traced here: 432 us
  Pallas kernels  428 us (99%)
    pallas_call x1, Pallas kernels, optimizer_step(): pl.pallas_call(step_kernel, out_shape=(pltpu.HBM((16, TOTAL - MOVED, 4, P...  383 us
    pallas_call x1, Pallas kernels, finish(): pl.pallas_call(finish_kernel, out_shape=tuple(shapes), in_specs=[any_spac...  34 us
    pallas_call x2, Pallas kernels, finish_far(): pl.pallas_call(functools.partial(far_kernel, other), out_shape=tuple((jax...  11.1 us
  transfers between devices with their start and end apart: 6, of which 1 were waited for; matrix products, arithmetic and copies ran while one was open for 0% of the time, Pallas kernels for 9%

profile of v1, /device:TPU:0, one launch (start us, length us, event | category | flops | bytes accessed | tf_op | source)
XLA Modules:
  0.0 432.4 jit_solution(12481411765434493726)
XLA Ops:
  0.7 382.9 %lamb_step.1 = (bf16[16,21,4,9216]{3,2,1,0:T(4,128)(2,1)}, bf16[4,15,4,3072]{3,2,1,0:T(4,128)(2,1)}, bf16[4,15,4,3072]{3,2,1,0:T(4,128)(2,1)}, bf16[4,15,4,3072]...) custom-call(bf16[3,2359296]{1,0:T(4,128)(2,1)} %bitcast.4, ...), custom_call_target="tpu_custom_call" | custom-call | tf_op jit(solution)/shard_map/lamb_step/pallas_call | solution.py:593
  383.6 1.3 collective-permute-start
  384.8 0.8 collective-permute-start.2
  385.6 0.6 collective-permute-start.4
  386.3 34.0 %finish.1 = (bf16[3,2359296]{1,0:T(4,128)(2,1)}, f32[3,147456]{1,0:T(4,128)}, f32[3,147456]{1,0:T(4,128)}, f32[3,147456]{1,0:T(4,128)}, bf16[3,2359296]{1,0:T(4,...) custom-call(bf16[16,21,4,9216]{3,2,1,0:T(4,128)(2,1)} %get-tuple-ele, ...), custom_call_target="tpu_custom_call" | custom-call | flops 999999995904 | bytes 100000000 | tf_op jit(solution)/shard_map/finish/pallas_call | solution.py:546
  420.3 0.0 collective-permute-done.refs_0_
  420.3 0.0 collective-permute-start.1
  420.3 0.0 collective-permute-done.2.refs_1_
  420.3 0.5 collective-permute-start.3
  420.8 0.0 collective-permute-done.4.refs_2_
  420.8 0.1 collective-permute-start.5
  420.9 6.7 %shard_map.279 = (bf16[3,2359296]{1,0:T(4,128)(2,1)}, bf16[3,2359296]{1,0:T(4,128)(2,1)}) custom-call(bf16[4,15,4,3072]{3,2,1,0:T(4,128)(2,1)} %collective-permute-done.refs_0_, bf16[4,15,4,3072]{3,2,1,0:T(4,128)(2,1)} %collective-permute-done.2.refs_1_, ...), custom_call_target="tpu_custom_call", output_to_operand_aliasing={{0}: (3, {}), {1}: (4, {})} | custom-call | flops 99999997952 | bytes 10000000 | tf_op jit(solution)/shard_map/pallas_call | solution.py:570
  427.5 0.0 collective-permute-done.1.refs_0_
  427.6 0.0 collective-permute-done.3.refs_1_
  427.6 0.4 collective-permute-done.5.refs_2_
  428.0 4.4 %shard_map.280 = (bf16[3,2359296]{1,0:T(4,128)(2,1)}, bf16[3,2359296]{1,0:T(4,128)(2,1)}) custom-call(bf16[4,15,4,3072]{3,2,1,0:T(4,128)(2,1)S(1)} %collective-permute-done.1.refs_0_, bf16[4,15,4,3072]{3,2,1,0:T(4,128)(2,1)S(1)} %collective-permute-done.3.refs_1_, ...), custom_call_target="tpu_custom_call", output_to_operand_aliasing={{0}: (3, {}), {1}: (4, {})} | custom-call | flops 99999997952 | bytes 10000000 | tf_op jit(solution)/shard_map/pallas_call | solution.py:570
Async XLA Ops:
  383.6 36.7 %collective-permute-start = (bf16[4,15,4,3072]{3,2,1,0:T(4,128)(2,1)}, bf16[4,15,4,3072]{3,2,1,0:T(4,128)(2,1)}, u32[]{:S(2)}, u32[]{:S(2)}) collective-permute-start(bf16[4,15,4,3072]{3,2,1,0:T(4,128)(2,1)} %get-tuple-element.45.near_0), channel_id=1, source_target_pairs={{0,8},{1,9},{2,10},{3,11},{4,12},{5,13},{6,14},{7,15},{8,0},{9,1},... | collective-permute-start | bytes 4423688 | tf_op jit(solution)/shard_map/ppermute | solution.py:625
  384.8 35.5 %collective-permute-start.2 = (bf16[4,15,4,3072]{3,2,1,0:T(4,128)(2,1)}, bf16[4,15,4,3072]{3,2,1,0:T(4,128)(2,1)}, u32[]{:S(2)}, u32[]{:S(2)}) collective-permute-start(bf16[4,15,4,3072]{3,2,1,0:T(4,128)(2,1)} %get-tuple-element.46.near_1), channel_id=1, source_target_pairs={{0,2},{1,3},{2,0},{3,1},{4,6},{5,7},{6,4},{7,5},{8,10},{9,11},{10,... | collective-permute-start | bytes 4423688 | tf_op jit(solution)/shard_map/ppermute | solution.py:625
  385.6 35.2 %collective-permute-start.4 = (bf16[4,15,4,3072]{3,2,1,0:T(4,128)(2,1)}, bf16[4,15,4,3072]{3,2,1,0:T(4,128)(2,1)}, u32[]{:S(2)}, u32[]{:S(2)}) collective-permute-start(bf16[4,15,4,3072]{3,2,1,0:T(4,128)(2,1)} %get-tuple-element.47.near_2), channel_id=1, source_target_pairs={{0,4},{1,5},{2,6},{3,7},{4,0},{5,1},{6,2},{7,3},{8,12},{9,13},{10,... | collective-permute-start | bytes 4423688 | tf_op jit(solution)/shard_map/ppermute | solution.py:625
  420.3 7.3 %collective-permute-start.1 = (bf16[4,15,4,3072]{3,2,1,0:T(4,128)(2,1)}, bf16[4,15,4,3072]{3,2,1,0:T(4,128)(2,1)S(1)}, u32[]{:S(2)}, u32[]{:S(2)}) collective-permute-start(bf16[4,15,4,3072]{3,2,1,0:T(4,128)(2,1)} %collective-permute-done.refs_0_), channel_id=1, source_target_pairs={{0,1},{1,0},{2,3},{3,2},{4,5},{5,4},{6,7},{7,6},{8,9},{9,8},{10,11... | collective-permute-start | bytes 4423688 | tf_op jit(solution)/shard_map/ppermute | solution.py:629
  420.3 7.2 %collective-permute-start.3 = (bf16[4,15,4,3072]{3,2,1,0:T(4,128)(2,1)}, bf16[4,15,4,3072]{3,2,1,0:T(4,128)(2,1)S(1)}, u32[]{:S(2)}, u32[]{:S(2)}) collective-permute-start(bf16[4,15,4,3072]{3,2,1,0:T(4,128)(2,1)} %collective-permute-done.2.refs_1_), channel_id=1, source_target_pairs={{0,1},{1,0},{2,3},{3,2},{4,5},{5,4},{6,7},{7,6},{8,9},{9,8},{10,11... | collective-permute-start | bytes 4423688 | tf_op jit(solution)/shard_map/ppermute | solution.py:629
  420.8 7.2 %collective-permute-start.5 = (bf16[4,15,4,3072]{3,2,1,0:T(4,128)(2,1)}, bf16[4,15,4,3072]{3,2,1,0:T(4,128)(2,1)S(1)}, u32[]{:S(2)}, u32[]{:S(2)}) collective-permute-start(bf16[4,15,4,3072]{3,2,1,0:T(4,128)(2,1)} %collective-permute-done.4.refs_2_), channel_id=1, source_target_pairs={{0,1},{1,0},{2,3},{3,2},{4,5},{5,4},{6,7},{7,6},{8,9},{9,8},{10,11... | collective-permute-start | bytes 4423688 | tf_op jit(solution)/shard_map/ppermute | solution.py:629

commit v2 on v1

--- a/solution.py
+++ b/solution.py
@@ -30,11 +30,12 @@
 MOVED = 15
 STEP_VMEM = 28 << 20
 LAST_VMEM = 13 << 20
-FAR_VMEM = 6 << 20
+FAR_VMEM = 9 << 20
 PACK_AT = 17
 GROUP = 3
-DEPTH = 12
-RING = 4
+DEPTH = 9
+RING = 6
+FAR_RING = 9
 ORDERS = ((0, 1, 2), (1, 2, 0), (2, 0, 1))
 
 
@@ -415,6 +416,7 @@
     def __init__(self, sources, far, outs, buffers):
         self.sources, self.far, self.outs = sources, far, outs
         self.full, self.rows, self.store_sem = buffers
+        self.depth = self.full.shape[0]
         self.groups = MOVED // GROUP
         self.steps = 4 * self.groups
         me = lax.axis_index("data")
@@ -422,7 +424,7 @@
         self.bits = ((me // 2) % 2, (me // 4) % 2, (me // 8) % 2)
 
     def store(self, step):
-        slot = lax.rem(step, RING)
+        slot = lax.rem(step, self.depth)
         j, group = step // self.groups, lax.rem(step, self.groups)
         for i, (_, k, other) in enumerate(self.sources):
             rel = [0, 0, 0]
@@ -440,9 +442,9 @@
 
     def run(self):
         def body(step, _):
-            slot = lax.rem(step, RING)
-
-            @pl.when(step >= RING)
+            slot = lax.rem(step, self.depth)
+
+            @pl.when(step >= self.depth)
             def _():
                 wait_for(self.full.at[slot], self.store_sem.at[slot])
 
@@ -456,12 +458,12 @@
         lax.fori_loop(0, self.steps, body, 0)
 
     def drain(self):
-        for slot in range(RING):
+        for slot in range(self.depth):
             wait_for(self.full.at[slot], self.store_sem.at[slot])
 
     @staticmethod
-    def scratch(count):
-        return [pltpu.VMEM((RING, count, 3, CHUNK), jnp.bfloat16), pltpu.VMEM((GROUP, 3, INNER), jnp.float32), pltpu.SemaphoreType.DMA((RING,))]
+    def scratch(count, depth):
+        return [pltpu.VMEM((depth, count, 3, CHUNK), jnp.bfloat16), pltpu.VMEM((GROUP, 3, INNER), jnp.float32), pltpu.SemaphoreType.DMA((depth,))]
 
 
 def finish_kernel(gathered, near_0, near_1, near_2, mate, wv, mv, vv, *refs):
@@ -551,7 +553,7 @@
         scratch_shapes=[
             pltpu.VMEM((DEPTH, GROUP, 4, PACKED), bf16), pltpu.VMEM((DEPTH, 3, GROUP * CHUNK), bf16),
             dma((DEPTH,)), dma((DEPTH,)), dma((3,)),
-        ] + MovedRing.scratch(6),
+        ] + MovedRing.scratch(6, RING),
         compiler_params=pltpu.CompilerParams(vmem_limit_bytes=LAST_VMEM),
         cost_estimate=pl.CostEstimate(flops=10 ** 12, bytes_accessed=10 ** 8, transcendentals=0),
         name="finish",
@@ -572,7 +574,7 @@
         out_shape=tuple(jax.ShapeDtypeStruct(x.shape, x.dtype) for x in copies),
         in_specs=[pl.BlockSpec(memory_space=pltpu.VMEM)] * 3 + [any_space] * 2,
         out_specs=(any_space,) * 2,
-        scratch_shapes=MovedRing.scratch(3),
+        scratch_shapes=MovedRing.scratch(3, FAR_RING),
         input_output_aliases={3: 0, 4: 1},
         compiler_params=pltpu.CompilerParams(vmem_limit_bytes=FAR_VMEM),
         cost_estimate=pl.CostEstimate(flops=10 ** 11, bytes_accessed=10 ** 7, transcendentals=0),

time: 433 us -> 431 us (level)
  no operation moved by 1% of the time
where the time goes in v2:
time: 431 us
  Pallas kernels  425 us (99%)
    pallas_call x1, Pallas kernels, optimizer_step(): pl.pallas_call(step_kernel, out_shape=(pltpu.HBM((16, TOTAL - MOVED, 4, P...  383 us
    pallas_call x1, Pallas kernels, finish(): pl.pallas_call(finish_kernel, out_shape=tuple(shapes), in_specs=[any_spac...  33.5 us
  transfers between devices with their start and end apart: 6, of which 1 were waited for; matrix products, arithmetic and copies ran while one was open for 0% of the time, Pallas kernels for 9%

profile of v2, /device:TPU:0, one launch (start us, length us, event | category | flops | bytes accessed | tf_op | source)
XLA Modules:
  0.0 430.6 jit_solution(14469091368547002322)
XLA Ops:
  0.7 382.9 %lamb_step.1 = (bf16[16,21,4,9216]{3,2,1,0:T(4,128)(2,1)}, bf16[4,15,4,3072]{3,2,1,0:T(4,128)(2,1)}, bf16[4,15,4,3072]{3,2,1,0:T(4,128)(2,1)}, bf16[4,15,4,3072]...) custom-call(bf16[3,2359296]{1,0:T(4,128)(2,1)} %bitcast.4, ...), custom_call_target="tpu_custom_call" | custom-call | tf_op jit(solution)/shard_map/lamb_step/pallas_call | solution.py:595
  383.6 1.3 collective-permute-start
  384.8 0.8 collective-permute-start.2
  385.6 0.6 collective-permute-start.4
  386.3 33.5 %finish.1 = (bf16[3,2359296]{1,0:T(4,128)(2,1)}, f32[3,147456]{1,0:T(4,128)}, f32[3,147456]{1,0:T(4,128)}, f32[3,147456]{1,0:T(4,128)}, bf16[3,2359296]{1,0:T(4,...) custom-call(bf16[16,21,4,9216]{3,2,1,0:T(4,128)(2,1)} %get-tuple-ele, ...), custom_call_target="tpu_custom_call" | custom-call | flops 999999995904 | bytes 100000000 | tf_op jit(solution)/shard_map/finish/pallas_call | solution.py:548
  419.7 0.0 collective-permute-done.refs_0_
  419.7 0.0 collective-permute-start.1
  419.8 0.0 collective-permute-done.2.refs_1_
  419.8 0.5 collective-permute-start.3
  420.3 0.0 collective-permute-done.4.refs_2_
  420.3 0.1 collective-permute-start.5
  420.4 5.3 %shard_map.279 = (bf16[3,2359296]{1,0:T(4,128)(2,1)}, bf16[3,2359296]{1,0:T(4,128)(2,1)}) custom-call(bf16[4,15,4,3072]{3,2,1,0:T(4,128)(2,1)} %collective-permute-done.refs_0_, bf16[4,15,4,3072]{3,2,1,0:T(4,128)(2,1)} %collective-permute-done.2.refs_1_, ...), custom_call_target="tpu_custom_call", output_to_operand_aliasing={{0}: (3, {}), {1}: (4, {})} | custom-call | flops 99999997952 | bytes 10000000 | tf_op jit(solution)/shard_map/pallas_call | solution.py:572
  425.7 0.0 collective-permute-done.1.refs_0_
  425.7 0.0 collective-permute-done.3.refs_1_
  425.7 1.7 collective-permute-done.5.refs_2_
  427.5 3.1 shard_map.280
Async XLA Ops:
  383.6 36.2 %collective-permute-start = (bf16[4,15,4,3072]{3,2,1,0:T(4,128)(2,1)}, bf16[4,15,4,3072]{3,2,1,0:T(4,128)(2,1)}, u32[]{:S(2)}, u32[]{:S(2)}) collective-permute-start(bf16[4,15,4,3072]{3,2,1,0:T(4,128)(2,1)} %get-tuple-element.45.near_0), channel_id=1, source_target_pairs={{0,8},{1,9},{2,10},{3,11},{4,12},{5,13},{6,14},{7,15},{8,0},{9,1},... | collective-permute-start | bytes 4423688 | tf_op jit(solution)/shard_map/ppermute | solution.py:627
  384.8 35.0 %collective-permute-start.2 = (bf16[4,15,4,3072]{3,2,1,0:T(4,128)(2,1)}, bf16[4,15,4,3072]{3,2,1,0:T(4,128)(2,1)}, u32[]{:S(2)}, u32[]{:S(2)}) collective-permute-start(bf16[4,15,4,3072]{3,2,1,0:T(4,128)(2,1)} %get-tuple-element.46.near_1), channel_id=1, source_target_pairs={{0,2},{1,3},{2,0},{3,1},{4,6},{5,7},{6,4},{7,5},{8,10},{9,11},{10,... | collective-permute-start | bytes 4423688 | tf_op jit(solution)/shard_map/ppermute | solution.py:627
  385.6 34.7 %collective-permute-start.4 = (bf16[4,15,4,3072]{3,2,1,0:T(4,128)(2,1)}, bf16[4,15,4,3072]{3,2,1,0:T(4,128)(2,1)}, u32[]{:S(2)}, u32[]{:S(2)}) collective-permute-start(bf16[4,15,4,3072]{3,2,1,0:T(4,128)(2,1)} %get-tuple-element.47.near_2), channel_id=1, source_target_pairs={{0,4},{1,5},{2,6},{3,7},{4,0},{5,1},{6,2},{7,3},{8,12},{9,13},{10,... | collective-permute-start | bytes 4423688 | tf_op jit(solution)/shard_map/ppermute | solution.py:627
  419.7 6.0 %collective-permute-start.1 = (bf16[4,15,4,3072]{3,2,1,0:T(4,128)(2,1)}, bf16[4,15,4,3072]{3,2,1,0:T(4,128)(2,1)S(1)}, u32[]{:S(2)}, u32[]{:S(2)}) collective-permute-start(bf16[4,15,4,3072]{3,2,1,0:T(4,128)(2,1)} %collective-permute-done.refs_0_), channel_id=1, source_target_pairs={{0,1},{1,0},{2,3},{3,2},{4,5},{5,4},{6,7},{7,6},{8,9},{9,8},{10,11... | collective-permute-start | bytes 4423688 | tf_op jit(solution)/shard_map/ppermute | solution.py:631
  419.8 5.9 %collective-permute-start.3 = (bf16[4,15,4,3072]{3,2,1,0:T(4,128)(2,1)}, bf16[4,15,4,3072]{3,2,1,0:T(4,128)(2,1)S(1)}, u32[]{:S(2)}, u32[]{:S(2)}) collective-permute-start(bf16[4,15,4,3072]{3,2,1,0:T(4,128)(2,1)} %collective-permute-done.2.refs_1_), channel_id=1, source_target_pairs={{0,1},{1,0},{2,3},{3,2},{4,5},{5,4},{6,7},{7,6},{8,9},{9,8},{10,11... | collective-permute-start | bytes 4423688 | tf_op jit(solution)/shard_map/ppermute | solution.py:631
  420.3 7.2 %collective-permute-start.5 = (bf16[4,15,4,3072]{3,2,1,0:T(4,128)(2,1)}, bf16[4,15,4,3072]{3,2,1,0:T(4,128)(2,1)S(1)}, u32[]{:S(2)}, u32[]{:S(2)}) collective-permute-start(bf16[4,15,4,3072]{3,2,1,0:T(4,128)(2,1)} %collective-permute-done.4.refs_2_), channel_id=1, source_target_pairs={{0,1},{1,0},{2,3},{3,2},{4,5},{5,4},{6,7},{7,6},{8,9},{9,8},{10,11... | collective-permute-start | bytes 4423688 | tf_op jit(solution)/shard_map/ppermute | solution.py:631
